TPU v7x, 32 devices: a whole 2x2x4 slice. The times are simulated.
32 devices in a mesh: img: 8 (over z, x), row: 4 (over y, core).
Axes of the slice: x: 2, y: 2, z: 4, core: 2. Of those that a mesh axis runs over, the one named last changes fastest.
Arguments:
- tokens: bfloat16 [8, 32, 128, 1024], P('img', 'row'), may hold values from -14 to 14
- proj_weight: bfloat16 [1024, 256], replicated, may hold values from -0.1875 to 0.1875
- proj_bias: float32 [256], replicated, may hold values from -3 to 3
- conv_weight: bfloat16 [4, 3, 3, 256, 256], replicated, may hold values from -0.125 to 0.125
- bn_gain: float32 [4, 256], replicated, may hold values from 0.1 to 1.9
- bn_bias: float32 [4, 256], replicated, may hold values from -3 to 3
Outputs:
- joining_out: bfloat16 [8, 32, 128, 256], P('img', 'row')
All inputs are finite; a program needn't handle non-finite values.
Results may differ from a plain program's by a relative error of at most 0.0071.
Values may be sent and summed in bfloat16 or wider, within the bound.
A program may use at most 64 MiB of HBM per device.

v0:
```python
import functools

import jax
import jax.numpy as jnp
from jax import lax
from jax.experimental import pallas as pl
from jax.experimental.pallas import tpu as pltpu
from jax.sharding import PartitionSpec as P

epsilon = 1e-05
MESH = pl.DeviceIdType.MESH
F32 = jnp.float32
BF16 = jnp.bfloat16
PLAN = ("flat",)
UNROLL = 0
ROWS = 2
VMEM_LIMIT = 62 * 1024 * 1024


def kernel(
    imgs,
    strips,
    height,
    cols,
    tokens_ref,
    pw_ref,
    pb_ref,
    cw_ref,
    gain_ref,
    bias_ref,
    out_ref,
    tok,
    pw,
    cw,
    feat,
    joined,
    xcat,
    raw,
    stats,
    peers,
    load_sem,
    weight_sem,
    halo_send,
    halo_recv,
    stat_send,
    stat_recv,
):
    count = imgs * strips
    width = feat.shape[-1]
    cells = height * cols
    me_img, me_row = lax.axis_index("img"), lax.axis_index("row")
    me = me_img * strips + me_row
    has_up, has_down = me_row > 0, me_row < strips - 1

    def peer(distance):
        target = lax.rem(me + distance, count)
        return {"img": target // strips, "row": lax.rem(target, strips)}

    def row_peer(distance):
        return {"img": me_img, "row": lax.rem(me_row + distance, strips)}

    def img_peer(distance):
        return {"img": lax.rem(me_img + distance, imgs), "row": me_row}

    def core_peer(distance):
        return {"img": me_img, "row": me_row + 1 - 2 * lax.rem(me_row, 2)}

    def chip_peer(distance):
        chips = strips // 2
        target = lax.rem(me_img * chips + me_row // 2 + distance, imgs * chips)
        return {"img": target // chips, "row": 2 * lax.rem(target, chips) + lax.rem(me_row, 2)}

    peer_of = {
        "flat": peer, "row": row_peer, "img": img_peer, "core": core_peer, "chip": chip_peer
    }

    def rows(first, number):
        return pl.ds(first * cols, number * cols)

    loads = [
        pltpu.make_async_copy(pw_ref, pw, load_sem.at[0]),
        pltpu.make_async_copy(tokens_ref.at[rows(0, 1)], tok.at[rows(0, 1)], load_sem.at[1]),
        pltpu.make_async_copy(
            tokens_ref.at[rows(height - 1, 1)], tok.at[rows(height - 1, 1)], load_sem.at[2]
        ),
        pltpu.make_async_copy(
            tokens_ref.at[rows(1, height - 2)], tok.at[rows(1, height - 2)], load_sem.at[3]
        ),
    ]
    weights = [
        pltpu.make_async_copy(
            cw_ref.at[pl.ds(3 * k, 3)], cw.at[pl.ds(3 * k, 3)], weight_sem.at[k]
        )
        for k in range(4)
    ]
    for load in loads:
        load.start()
    weights[0].start()

    barrier = pltpu.get_barrier_semaphore()

    @pl.loop(1, count)
    def _(distance):
        pl.semaphore_signal(barrier, inc=1, device_id=peer(distance), device_id_type=MESH)

    for k in range(1, 4):
        weights[k].start()

    @pl.when(jnp.logical_not(has_up))
    def _():
        xcat[rows(0, 1), :] = jnp.zeros((cols, 3 * width), BF16)

    @pl.when(jnp.logical_not(has_down))
    def _():
        xcat[rows(height + 1, 1), :] = jnp.zeros((cols, 3 * width), BF16)

    column = lax.broadcasted_iota(jnp.int32, (cols, width), 0)

    def span(row):
        return pl.ds(pl.multiple_of(row * cols, cols), cols)

    def put(row, value):
        at = span(row)
        xcat[at, 0:width] = jnp.where(column == 0, 0.0, pltpu.roll(value, 1, 0)).astype(BF16)
        xcat[at, width : 2 * width] = value.astype(BF16)
        xcat[at, 2 * width : 3 * width] = jnp.where(
            column == cols - 1, 0.0, pltpu.roll(value, cols - 1, 0)
        ).astype(BF16)

    def project(row):
        value = jnp.dot(tok[span(row), :], pw[...], preferred_element_type=F32) + pb_ref[...]
        value = value.astype(BF16)
        feat[span(row + 1), :] = value
        put(row + 1, jnp.maximum(value.astype(F32), 0.0))

    def halo(ref, phase):
        up = pltpu.make_async_remote_copy(
            src_ref=ref.at[rows(1, 1)],
            dst_ref=ref.at[rows(height + 1, 1)],
            send_sem=halo_send.at[phase, 0],
            recv_sem=halo_recv.at[phase, 1],
            device_id={"img": me_img, "row": jnp.maximum(me_row - 1, 0)},
            device_id_type=MESH,
        )
        down = pltpu.make_async_remote_copy(
            src_ref=ref.at[rows(height, 1)],
            dst_ref=ref.at[rows(0, 1)],
            send_sem=halo_send.at[phase, 1],
            recv_sem=halo_recv.at[phase, 0],
            device_id={"img": me_img, "row": jnp.minimum(me_row + 1, strips - 1)},
            device_id_type=MESH,
        )
        return up, down

    def send_halo(ref, phase):
        up, down = halo(ref, phase)

        @pl.when(has_up)
        def _():
            up.start()

        @pl.when(has_down)
        def _():
            down.start()

    def take_halo(ref, phase, top, bottom):
        up, down = halo(ref, phase)

        @pl.when(has_up)
        def _():
            down.wait_recv()
            top()

        @pl.when(has_down)
        def _():
            up.wait_recv()
            bottom()

    def end_halo(ref, phase):
        up, down = halo(ref, phase)

        @pl.when(has_up)
        def _():
            up.wait_send()

        @pl.when(has_down)
        def _():
            down.wait_send()

    def taps(k, first, number, which):
        return sum(
            jnp.dot(xcat[rows(first + dy, number), :], cw[3 * k + dy], preferred_element_type=F32)
            for dy in which
        )

    def moments(value):
        size = value.shape[0]
        first = jnp.sum(value, axis=0, keepdims=True)
        squares = jnp.sum(jnp.square(value - first / size), axis=0, keepdims=True)
        return first, squares, size

    def conv(k, first, number):
        value = taps(k, first, number, range(3))
        raw[k, rows(first + 1, number), :] = value
        return moments(value)

    def finish(k, first, dy):
        value = raw[k, rows(first + 1, 1), :] + taps(k, first, 1, (dy,))
        raw[k, rows(first + 1, 1), :] = value
        return moments(value)

    def stat_copy(k, stage, distance):
        return pltpu.make_async_remote_copy(
            src_ref=stats[stage].at[k],
            dst_ref=peers[stage].at[k, distance - 1],
            send_sem=stat_send.at[k, stage],
            recv_sem=stat_recv.at[k, stage],
            device_id=peer_of[PLAN[stage]](distance),
            device_id_type=MESH,
        )

    def spread_stat(k, stage):
        others = peers[stage].shape[1]
        if others <= UNROLL:
            for distance in range(1, others + 1):
                stat_copy(k, stage, distance).start()
        else:
            pl.loop(1, others + 1)(lambda distance: stat_copy(k, stage, distance).start())

    def send_stat(k, chunks):
        total = sum(chunk[0] for chunk in chunks)
        centre = total / cells
        squares = sum(
            chunk[1] + jnp.square(chunk[0] / chunk[2] - centre) * chunk[2] for chunk in chunks
        )
        stats[0][k] = jnp.concatenate([total, squares], axis=0)
        spread_stat(k, 0)

    def take_stat(k):
        size = cells
        for stage in range(len(PLAN)):
            buffer = peers[stage]
            others = buffer.shape[1]
            own = stats[stage][k]
            pltpu.make_async_copy(buffer.at[k], buffer.at[k], stat_recv.at[k, stage]).wait()
            every = buffer[k]
            total = jnp.sum(every, axis=0) + own
            even = total[0:1] / (others + 1)
            gaps = jnp.sum(jnp.square(every[:, 0, :] - even), axis=0, keepdims=True)
            gaps += jnp.square(own[0:1] - even)
            squares = total[1:2] + gaps / size
            size *= others + 1
            if stage + 1 < len(PLAN):
                stats[stage + 1][k] = jnp.concatenate([total[0:1], squares], axis=0)
                spread_stat(k, stage + 1)
        average = total[0:1] / size
        scale = lax.rsqrt(squares / size + epsilon) * gain_ref[pl.ds(k, 1), :]
        return average, scale, bias_ref[pl.ds(k, 1), :]

    def normed(k, row, norm):
        average, scale, shift = norm
        return (raw[k, span(row), :] - average) * scale + shift

    rim_first = [(0, 2), (height - 2, 2)]
    middle = [(first, 2) for first in range(2, height - 2, 2)]
    inside = [(first, 2) for first in range(1, height - 1, 2)]

    loads[0].wait()
    loads[1].wait()
    project(0)
    loads[2].wait()
    project(height - 1)
    pl.semaphore_wait(barrier, count - 1)
    send_halo(feat, 0)
    loads[3].wait()

    @pl.loop(1, height - 1, unroll=ROWS)
    def _(row):
        project(row)

    def feature_rim(row):
        put(row, jnp.maximum(feat[span(row), :].astype(F32), 0.0))

    weights[0].wait()
    chunks = [conv(0, first, number) for first, number in inside]
    raw[0, rows(1, 1), :] = taps(0, 0, 1, (1, 2))
    raw[0, rows(height, 1), :] = taps(0, height - 1, 1, (0, 1))
    take_halo(feat, 0, lambda: feature_rim(0), lambda: feature_rim(height + 1))
    chunks += [finish(0, 0, 0), finish(0, height - 1, 2)]
    send_halo(raw.at[0], 1)
    send_stat(0, chunks)

    def later_conv(k):
        weights[k].wait()
        chunks = [conv(k, first, number) for first, number in rim_first]
        if k < 3:
            send_halo(raw.at[k], k + 1)
        chunks += [conv(k, first, number) for first, number in middle]
        send_stat(k, chunks)

    def hidden(k):
        norm = take_stat(k)

        def one(row):
            put(row, jnp.maximum(normed(k, row, norm), 0.0))

        pl.loop(1, height + 1, unroll=ROWS)(one)
        take_halo(raw.at[k], k + 1, lambda: one(0), lambda: one(height + 1))

    hidden(0)
    later_conv(1)

    norm_1 = take_stat(1)

    def join(row, local):
        value = (feat[span(row), :].astype(F32) + normed(1, row, norm_1)).astype(BF16)
        if local:
            joined[span(row - 1), :] = value
        put(row, jnp.maximum(value.astype(F32), 0.0))

    pl.loop(1, height + 1, unroll=ROWS)(lambda row: join(row, True))
    take_halo(raw.at[1], 2, lambda: join(0, False), lambda: join(height + 1, False))
    later_conv(2)
    hidden(2)
    later_conv(3)
    norm_3 = take_stat(3)

    @pl.loop(0, height, unroll=ROWS)
    def _(row):
        value = joined[span(row), :].astype(F32) + normed(3, row + 1, norm_3)
        out_ref[span(row), :] = value.astype(BF16)

    end_halo(feat, 0)
    for k in range(3):
        end_halo(raw.at[k], k + 1)
    for k in range(4):
        for stage, buffer in enumerate(peers):
            pltpu.make_async_copy(buffer.at[k], buffer.at[k], stat_send.at[k, stage]).wait()


def solution(mesh):
    imgs, strips = mesh.shape["img"], mesh.shape["row"]

    def on_device(tokens, proj_weight, proj_bias, conv_weight, bn_gain, bn_bias):
        images, height, cols, embed = tokens.shape
        convs, taps, _, width, _ = conv_weight.shape
        assert images == 1 and height % 2 == 0 and height >= 4
        count = imgs * strips
        sizes = {"flat": count, "row": strips, "img": imgs, "core": 2, "chip": count // 2}
        cells = height * cols
        any_space = pl.BlockSpec(memory_space=pltpu.HBM)
        vmem = pl.BlockSpec(memory_space=pltpu.VMEM)
        out = pl.pallas_call(
            functools.partial(kernel, imgs, strips, height, cols),
            out_shape=jax.ShapeDtypeStruct((cells, width), BF16),
            in_specs=[any_space, any_space, vmem, any_space, vmem, vmem],
            out_specs=vmem,
            scratch_shapes=[
                pltpu.VMEM((cells, embed), BF16),
                pltpu.VMEM((embed, width), BF16),
                pltpu.VMEM((convs * taps, taps * width, width), BF16),
                pltpu.VMEM((cells + 2 * cols, width), BF16),
                pltpu.VMEM((cells, width), BF16),
                pltpu.VMEM((cells + 2 * cols, taps * width), BF16),
                pltpu.VMEM((convs, cells + 2 * cols, width), F32),
                [pltpu.VMEM((convs, 2, width), F32) for _ in PLAN],
                [pltpu.VMEM((convs, sizes[part] - 1, 2, width), F32) for part in PLAN],
                pltpu.SemaphoreType.DMA((4,)),
                pltpu.SemaphoreType.DMA((convs,)),
                pltpu.SemaphoreType.DMA((convs, 2)),
                pltpu.SemaphoreType.DMA((convs, 2)),
                pltpu.SemaphoreType.DMA((convs, len(PLAN))),
                pltpu.SemaphoreType.DMA((convs, len(PLAN))),
            ],
            compiler_params=pltpu.CompilerParams(
                collective_id=0, has_side_effects=True, vmem_limit_bytes=VMEM_LIMIT
            ),
        )(
            tokens.reshape(cells, embed),
            proj_weight,
            proj_bias.reshape(1, width),
            conv_weight.reshape(convs * taps, taps * width, width),
            bn_gain,
            bn_bias,
        )
        return out.reshape(images, height, cols, width)

    in_specs = (P("img", "row", None, None), P(), P(), P(), P(), P())
    return jax.shard_map(
        on_device,
        mesh=mesh,
        in_specs=in_specs,
        out_specs=P("img", "row", None, None),
        check_vma=False,
    )
```

profile of v0, /device:TPU:0, one launch (start us, length us, event | category | flops | bytes accessed | tf_op | source)
XLA Modules:
  0.0 39.1 jit_solution(4419550940015387843)
XLA Ops:
  0.0 37.2 %shard_map.64 = bf16[1024,256]{1,0:T(8,128)(2,1)} custom-call(bf16[1024,1024]{1,0:T(8,128)(2,1)} %bitcast.5, bf16[1024,256]{1,0:T(8,128)(2,1)} %pw_ref.1, f32[1,256]{1,0:T(1,128)} %bitcast.7, bf16[12,768,256]{2,1,0:T(8,128)(2,1)} %bitcast.4, f32[4,256]{1,0:T(4,128)} %gain_ref.1, f32[4,256]{1,0:T(4,128)} %bias_ref.1), custom_call_target="tpu_custom_call" | custom-call | tf_op jit(solution)/shard_map/pallas_call | solution.py:353
  37.2 1.9 %copy.8 = bf16[1,8,128,256]{3,2,1,0:T(8,128)(2,1)} copy(bf16[1,8,128,256]{3,2,1,0:T(8,128)(2,1)} %bitcast.6) | data formatting | bytes 1048576
where the time goes:
time: 39.3 us; the launch traced here: 39.1 us
  Pallas kernels  37.2 us (95%)
  local copies, waits for them, and re-layouts  1.87 us (5%)
    pallas_call x1, Pallas kernels, on_device(): pl.pallas_call(functools.partial(kernel, imgs, strips, height, cols), out...  37.2 us
    unnamed x1, local copies, waits for them, and re-layouts  1.87 us

commit v1 on v0

v1 whole, which is shorter than its diff:
```python
import functools

import jax
import jax.numpy as jnp
from jax import lax
from jax.experimental import pallas as pl
from jax.experimental.pallas import tpu as pltpu
from jax.sharding import PartitionSpec as P

epsilon = 1e-05
LOGICAL = pl.DeviceIdType.LOGICAL
F32 = jnp.float32
BF16 = jnp.bfloat16
STEP = 2
UNROLL = 63
VMEM_LIMIT = 40 * 1024 * 1024


def kernel(
    imgs,
    strips,
    height,
    cols,
    tokens_ref,
    pw_ref,
    pb_ref,
    cw_ref,
    gain_ref,
    bias_ref,
    out_ref,
    tok,
    pw,
    pb,
    cw,
    gain,
    bias,
    feat,
    joined,
    xcat,
    raw,
    rim_out,
    rim_in,
    stats,
    peers,
    load_sem,
    weight_sem,
    halo_send,
    halo_recv,
    stat_send,
    stat_recv,
):
    count = imgs * strips
    width = feat.shape[-1]
    cells = height * cols
    me_row = lax.axis_index("row")
    me = lax.axis_index("img") * strips + me_row
    has_up, has_down = me_row > 0, me_row < strips - 1
    above = me - jnp.where(has_up, 1, 0)
    below = me + jnp.where(has_down, 1, 0)

    def peer(distance):
        target = me + distance
        return jnp.where(target >= count, target - count, target)

    def rows(first, number):
        return pl.ds(first * cols, number * cols)

    loads = [
        pltpu.make_async_copy(pw_ref, pw, load_sem.at[0]),
        pltpu.make_async_copy(tokens_ref.at[rows(0, 1)], tok.at[rows(0, 1)], load_sem.at[1]),
        pltpu.make_async_copy(
            tokens_ref.at[rows(height - 1, 1)], tok.at[rows(1, 1)], load_sem.at[2]
        ),
        pltpu.make_async_copy(pb_ref, pb, load_sem.at[3]),
        pltpu.make_async_copy(
            tokens_ref.at[rows(1, height - 2)], tok.at[rows(2, height - 2)], load_sem.at[4]
        ),
        pltpu.make_async_copy(gain_ref, gain, load_sem.at[5]),
        pltpu.make_async_copy(bias_ref, bias, load_sem.at[6]),
    ]
    weights = [
        pltpu.make_async_copy(
            cw_ref.at[pl.ds(3 * k, 3)], cw.at[pl.ds(3 * k, 3)], weight_sem.at[k]
        )
        for k in range(4)
    ]
    for load in loads[:5]:
        load.start()

    barrier = pltpu.get_barrier_semaphore()

    @pl.loop(1, count)
    def _(distance):
        pl.semaphore_signal(
            barrier, inc=1, device_id=peer(distance), device_id_type=LOGICAL
        )

    for weight in weights:
        weight.start()
    for load in loads[5:]:
        load.start()

    @pl.when(jnp.logical_not(has_up))
    def _():
        feat[rows(0, 1), :] = jnp.zeros((cols, width), BF16)
        for k in range(3):
            rim_in[k, 0] = jnp.zeros((cols, width), BF16)

    @pl.when(jnp.logical_not(has_down))
    def _():
        feat[rows(height + 1, 1), :] = jnp.zeros((cols, width), BF16)
        for k in range(3):
            rim_in[k, 1] = jnp.zeros((cols, width), BF16)

    column = lax.broadcasted_iota(jnp.int32, (cols, width), 0)
    at_left, at_right = column == 0, column == cols - 1

    def put(row, value):
        at = rows(row, 1)
        xcat[at, 0:width] = jnp.where(at_left, 0.0, pltpu.roll(value, 1, 0)).astype(BF16)
        xcat[at, width : 2 * width] = value.astype(BF16)
        xcat[at, 2 * width : 3 * width] = jnp.where(
            at_right, 0.0, pltpu.roll(value, cols - 1, 0)
        ).astype(BF16)

    def project(slot, number, where):
        value = jnp.dot(tok[rows(slot, number), :], pw[...], preferred_element_type=F32)
        value = (value + pb[...]).astype(BF16)
        for i, row in enumerate(where):
            part = value[i * cols : (i + 1) * cols]
            feat[rows(row + 1, 1), :] = part
            put(row + 1, jnp.maximum(part.astype(F32), 0.0))

    def halo(phase, up_from, up_to, down_from, down_to):
        up = pltpu.make_async_remote_copy(
            src_ref=up_from,
            dst_ref=up_to,
            send_sem=halo_send.at[phase, 0],
            recv_sem=halo_recv.at[phase, 1],
            device_id=above,
            device_id_type=LOGICAL,
        )
        down = pltpu.make_async_remote_copy(
            src_ref=down_from,
            dst_ref=down_to,
            send_sem=halo_send.at[phase, 1],
            recv_sem=halo_recv.at[phase, 0],
            device_id=below,
            device_id_type=LOGICAL,
        )
        return up, down

    def feature_halo():
        return halo(
            0,
            feat.at[rows(1, 1)],
            feat.at[rows(height + 1, 1)],
            feat.at[rows(height, 1)],
            feat.at[rows(0, 1)],
        )

    def raw_halo(k):
        return halo(
            k + 1, rim_out.at[k, 0], rim_in.at[k, 1], rim_out.at[k, 1], rim_in.at[k, 0]
        )

    def send_halo(pair):
        up, down = pair

        @pl.when(has_up)
        def _():
            up.start()

        @pl.when(has_down)
        def _():
            down.start()

    def take_halo(pair):
        up, down = pair

        @pl.when(has_up)
        def _():
            down.wait_recv()

        @pl.when(has_down)
        def _():
            up.wait_recv()

    def end_halo(pair):
        up, down = pair

        @pl.when(has_up)
        def _():
            up.wait_send()

        @pl.when(has_down)
        def _():
            down.wait_send()

    def taps(k, first, number, which):
        return sum(
            jnp.dot(xcat[rows(first + dy, number), :], cw[3 * k + dy], preferred_element_type=F32)
            for dy in which
        )

    def fold(value):
        return jnp.sum(value.reshape(value.shape[0] // 8, 8, width), axis=0)

    class Moments:
        def add(self, value):
            if not hasattr(self, "pivot"):
                self.pivot = jnp.sum(fold(value), axis=0, keepdims=True) / value.shape[0]
                self.first = jnp.zeros((8, width), F32)
                self.second = jnp.zeros((8, width), F32)
            gap = value - self.pivot
            self.first += fold(gap)
            self.second += fold(jnp.square(gap))

        def total(self):
            first = jnp.sum(self.first, axis=0, keepdims=True)
            second = jnp.sum(self.second, axis=0, keepdims=True)
            return first + cells * self.pivot, second - jnp.square(first) / cells

    def stat_copy(k, distance):
        return pltpu.make_async_remote_copy(
            src_ref=stats.at[k],
            dst_ref=peers.at[k, distance - 1],
            send_sem=stat_send.at[k],
            recv_sem=stat_recv.at[k],
            device_id=peer(distance),
            device_id_type=LOGICAL,
        )

    def send_stat(k, moments):
        total, squares = moments.total()
        stats[k] = jnp.concatenate([total, squares], axis=0)
        if count - 1 <= UNROLL:
            for distance in range(1, count):
                stat_copy(k, distance).start()
        else:
            pl.loop(1, count)(lambda distance: stat_copy(k, distance).start())

    def take_stat(k):
        own = stats[k]
        pltpu.make_async_copy(peers.at[k], peers.at[k], stat_recv.at[k]).wait()
        every = peers[k]
        total = jnp.sum(every, axis=0) + own
        even = total[0:1] / count
        gaps = jnp.sum(jnp.square(every[:, 0, :] - even), axis=0, keepdims=True)
        gaps += jnp.square(own[0:1] - even)
        squares = total[1:2] + gaps / cells
        size = cells * count
        average = total[0:1] / size
        scale = lax.rsqrt(squares / size + epsilon) * gain[k : k + 1, :]
        return average, scale, bias[k : k + 1, :]

    def normed(k, row, norm):
        average, scale, shift = norm
        if row == 0:
            value = rim_in[k, 0].astype(F32)
        elif row == height + 1:
            value = rim_in[k, 1].astype(F32)
        else:
            value = raw[k, rows(row - 1, 1), :]
        return (value - average) * scale + shift

    def inside(row, value):
        if row == 0:
            return jnp.where(has_up, value, 0.0)
        if row == height + 1:
            return jnp.where(has_down, value, 0.0)
        return value

    def conv_stage(k, fill):
        weights[k].wait()
        moments = Moments()
        filled = 0
        for first in range(0, height, STEP):
            while filled < first + STEP + 2:
                fill(filled)
                filled += 1
            value = taps(k, first, STEP, range(3))
            raw[k, rows(first, STEP), :] = value
            if k < 3 and first == 0:
                rim_out[k, 0] = value[:cols].astype(BF16)
            if k < 3 and first + STEP == height:
                rim_out[k, 1] = value[-cols:].astype(BF16)
            moments.add(value)
        send_stat(k, moments)
        if k < 3:
            send_halo(raw_halo(k))

    loads[0].wait()
    loads[1].wait()
    loads[2].wait()
    loads[3].wait()
    project(0, 2, (0, height - 1))
    pl.semaphore_wait(barrier, count - 1)
    send_halo(feature_halo())
    loads[4].wait()
    for slot in range(2, height, 2):
        project(slot, 2, (slot - 1, slot))

    weights[0].wait()
    moments = Moments()
    for first in range(1, height - 1, 2):
        value = taps(0, first, 2, range(3))
        raw[0, rows(first, 2), :] = value
        moments.add(value)
    top = taps(0, 0, 1, (1, 2))
    bottom = taps(0, height - 1, 1, (0, 1))
    raw[0, rows(0, 1), :] = top
    raw[0, rows(height - 1, 1), :] = bottom
    take_halo(feature_halo())
    put(0, jnp.maximum(feat[rows(0, 1), :].astype(F32), 0.0))
    put(height + 1, jnp.maximum(feat[rows(height + 1, 1), :].astype(F32), 0.0))
    top = raw[0, rows(0, 1), :] + taps(0, 0, 1, (0,))
    bottom = raw[0, rows(height - 1, 1), :] + taps(0, height - 1, 1, (2,))
    for side, row, value in ((0, 0, top), (1, height - 1, bottom)):
        raw[0, rows(row, 1), :] = value
        rim_out[0, side] = value.astype(BF16)
        moments.add(value)
    send_stat(0, moments)
    send_halo(raw_halo(0))
    loads[5].wait()
    loads[6].wait()

    def hidden(k):
        norm = take_stat(k)
        take_halo(raw_halo(k))

        def fill(row):
            put(row, inside(row, jnp.maximum(normed(k, row, norm), 0.0)))

        return fill

    conv_stage(1, hidden(0))

    norm_1 = take_stat(1)
    take_halo(raw_halo(1))

    def join(row):
        value = (feat[rows(row, 1), :].astype(F32) + normed(1, row, norm_1)).astype(BF16)
        if 1 <= row <= height:
            joined[rows(row - 1, 1), :] = value
        put(row, inside(row, jnp.maximum(value.astype(F32), 0.0)))

    conv_stage(2, join)
    conv_stage(3, hidden(2))
    norm_3 = take_stat(3)

    for row in range(height):
        value = joined[rows(row, 1), :].astype(F32) + normed(3, row + 1, norm_3)
        out_ref[rows(row, 1), :] = value.astype(BF16)

    end_halo(feature_halo())
    for k in range(3):
        end_halo(raw_halo(k))
    for k in range(4):
        pltpu.make_async_copy(peers.at[k], peers.at[k], stat_send.at[k]).wait()


def solution(mesh):
    imgs, strips = mesh.shape["img"], mesh.shape["row"]

    def on_device(tokens, proj_weight, proj_bias, conv_weight, bn_gain, bn_bias):
        images, height, cols, embed = tokens.shape
        convs, taps, _, width, _ = conv_weight.shape
        assert images == 1 and height % 2 == 0 and height >= 4
        count = imgs * strips
        cells = height * cols
        hbm = pl.BlockSpec(memory_space=pltpu.HBM)
        vmem = pl.BlockSpec(memory_space=pltpu.VMEM)
        operands = [
            tokens.reshape(cells, embed),
            proj_weight,
            proj_bias.reshape(1, width),
            conv_weight.reshape(convs * taps, taps * width, width),
            bn_gain,
            bn_bias,
        ]
        out = pl.pallas_call(
            functools.partial(kernel, imgs, strips, height, cols),
            out_shape=pltpu.VMEM((cells, width), BF16),
            in_specs=[hbm] * 6,
            out_specs=vmem,
            scratch_shapes=[
                pltpu.VMEM((cells, embed), BF16),
                pltpu.VMEM((embed, width), BF16),
                pltpu.VMEM((1, width), F32),
                pltpu.VMEM((convs * taps, taps * width, width), BF16),
                pltpu.VMEM((convs, width), F32),
                pltpu.VMEM((convs, width), F32),
                pltpu.VMEM((cells + 2 * cols, width), BF16),
                pltpu.VMEM((cells, width), BF16),
                pltpu.VMEM((cells + 2 * cols, taps * width), BF16),
                pltpu.VMEM((convs, cells, width), F32),
                pltpu.VMEM((convs - 1, 2, cols, width), BF16),
                pltpu.VMEM((convs - 1, 2, cols, width), BF16),
                pltpu.VMEM((convs, 2, width), F32),
                pltpu.VMEM((convs, count - 1, 2, width), F32),
                pltpu.SemaphoreType.DMA((7,)),
                pltpu.SemaphoreType.DMA((convs,)),
                pltpu.SemaphoreType.DMA((convs, 2)),
                pltpu.SemaphoreType.DMA((convs, 2)),
                pltpu.SemaphoreType.DMA((convs,)),
                pltpu.SemaphoreType.DMA((convs,)),
            ],
            compiler_params=pltpu.CompilerParams(
                collective_id=0, has_side_effects=True, vmem_limit_bytes=VMEM_LIMIT
            ),
        )(*[pltpu.with_memory_space_constraint(x, pltpu.HBM) for x in operands])
        return out.reshape(images, height, cols, width)

    in_specs = (P("img", "row", None, None), P(), P(), P(), P(), P())
    return jax.shard_map(
        on_device,
        mesh=mesh,
        in_specs=in_specs,
        out_specs=P("img", "row", None, None),
        check_vma=False,
    )
```

time: 39.3 us -> 34.8 us (0.89)
  Pallas kernels: 37.2 us -> 33.9 us
  local copies, waits for them, and re-layouts: 1.87 us -> 0.8 us
    pallas_call x1, Pallas kernels: 37.2 us -> 33.9 us  [on_device(): pl.pallas_call(functools.partial(kernel, imgs, strips, height, cols), out...]
    unnamed x1, local copies, waits for them, and re-layouts: 1.87 us -> 0.8 us
where the time goes in v1:
time: 34.8 us; the launch traced here: 34.7 us
  Pallas kernels  33.9 us (97%)
  local copies, waits for them, and re-layouts  0.8 us (2%)
    pallas_call x1, Pallas kernels, on_device(): pl.pallas_call(functools.partial(kernel, imgs, strips, height, cols), out...  33.9 us
    unnamed x1, local copies, waits for them, and re-layouts  0.8 us

profile of v1, /device:TPU:0, one launch (start us, length us, event | category | flops | bytes accessed | tf_op | source)
XLA Modules:
  0.0 34.7 jit_solution(11379586486407054438)
XLA Ops:
  0.0 33.9 %shard_map.64 = bf16[1024,256]{1,0:T(8,128)(2,1)S(1)} custom-call(bf16[1024,1024]{1,0:T(8,128)(2,1)} %bitcast.6, bf16[1024,256]{1,0:T(8,128)(2,1)} %pw_ref.1, f32[1,256]{1,0:T(1,128)} %bitcast.7, bf16[12,768,256]{2,1,0:T(8,128)(2,1)} %bitcast.5, f32[4,256]{1,0:T(4,128)} %gain_ref.1, f32[4,256]{1,0:T(4,128)} %bias_ref.1), custom_call_target="tpu_custom_call" | custom-call | tf_op jit(solution)/shard_map/pallas_call | solution.py:382
  33.9 0.8 %copy.8 = bf16[1,8,128,256]{3,2,1,0:T(8,128)(2,1)} copy(bf16[1,8,128,256]{3,2,1,0:T(8,128)(2,1)S(1)} %bitcast.4) | data formatting | bytes 1048576

commit v2 on v1

--- a/solution.py
+++ b/solution.py
@@ -14,6 +14,10 @@
 STEP = 2
 UNROLL = 63
 VMEM_LIMIT = 40 * 1024 * 1024
+
+
+def bits_of(count):
+    return [2**b for b in range(count.bit_length() - 1)]
 
 
 def kernel(
@@ -48,6 +52,8 @@
     halo_recv,
     stat_send,
     stat_recv,
+    near,
+    everyone,
 ):
     count = imgs * strips
     width = feat.shape[-1]
@@ -58,9 +64,17 @@
     above = me - jnp.where(has_up, 1, 0)
     below = me + jnp.where(has_down, 1, 0)
 
+    flips = [bit - 2 * bit * lax.rem(me // bit, 2) for bit in bits_of(count)]
+
     def peer(distance):
-        target = me + distance
-        return jnp.where(target >= count, target - count, target)
+        if isinstance(distance, int):
+            return me + sum(flip for b, flip in enumerate(flips) if distance >> b & 1)
+        return me + sum(flip * lax.rem(distance // 2**b, 2) for b, flip in enumerate(flips))
+
+    half = count // 2
+    odd = lax.rem(me_row, 2)
+    is_odd, is_even = odd == 1, odd == 0
+    partner = me + 1 - 2 * odd
 
     def rows(first, number):
         return pl.ds(first * cols, number * cols)
@@ -84,21 +98,39 @@
         )
         for k in range(4)
     ]
-    for load in loads[:5]:
+    for load in loads[:4]:
         load.start()
 
     barrier = pltpu.get_barrier_semaphore()
 
-    @pl.loop(1, count)
+    def greet(device):
+        pl.semaphore_signal(barrier, inc=1, device_id=device, device_id_type=LOGICAL)
+
+    @pl.when(is_odd)
+    def _():
+        greet(partner)
+
+        @pl.when(has_down)
+        def _():
+            greet(below)
+
+    @pl.when(jnp.logical_and(is_even, me_row >= 2))
+    def _():
+        greet(me - 2)
+
+    @pl.loop(1, half)
     def _(distance):
-        pl.semaphore_signal(
-            barrier, inc=1, device_id=peer(distance), device_id_type=LOGICAL
-        )
-
+        greet(peer(2 * (half - distance)) + 1 - odd)
+
+    @pl.when(is_even)
+    def _():
+        greet(partner)
+
+    loads[4].start(priority=1)
     for weight in weights:
-        weight.start()
+        weight.start(priority=1)
     for load in loads[5:]:
-        load.start()
+        load.start(priority=1)
 
     @pl.when(jnp.logical_not(has_up))
     def _():
@@ -127,9 +159,10 @@
         value = jnp.dot(tok[rows(slot, number), :], pw[...], preferred_element_type=F32)
         value = (value + pb[...]).astype(BF16)
         for i, row in enumerate(where):
-            part = value[i * cols : (i + 1) * cols]
-            feat[rows(row + 1, 1), :] = part
-            put(row + 1, jnp.maximum(part.astype(F32), 0.0))
+            feat[rows(row + 1, 1), :] = value[i * cols : (i + 1) * cols]
+
+    def activate(row):
+        put(row, jnp.maximum(feat[rows(row, 1), :].astype(F32), 0.0))
 
     def halo(phase, up_from, up_to, down_from, down_to):
         up = pltpu.make_async_remote_copy(
@@ -235,10 +268,10 @@
         total, squares = moments.total()
         stats[k] = jnp.concatenate([total, squares], axis=0)
         if count - 1 <= UNROLL:
-            for distance in range(1, count):
+            for distance in range(count - 1, 0, -1):
                 stat_copy(k, distance).start()
         else:
-            pl.loop(1, count)(lambda distance: stat_copy(k, distance).start())
+            pl.loop(1, count)(lambda distance: stat_copy(k, count - distance).start())
 
     def take_stat(k):
         own = stats[k]
@@ -295,11 +328,25 @@
     loads[2].wait()
     loads[3].wait()
     project(0, 2, (0, height - 1))
-    pl.semaphore_wait(barrier, count - 1)
+
+    @pl.when(is_even)
+    def _():
+        beside = jnp.where(me_row >= 2, 1, 0) + jnp.where(me_row + 2 < strips, 1, 0)
+        pl.semaphore_wait(barrier, 1 + beside)
+        pl.semaphore_signal(near, inc=1, device_id=partner, device_id_type=LOGICAL)
+
+    @pl.when(is_odd)
+    def _():
+        pl.semaphore_wait(near, 1)
+
     send_halo(feature_halo())
     loads[4].wait()
+    activate(1)
+    activate(height)
     for slot in range(2, height, 2):
         project(slot, 2, (slot - 1, slot))
+        activate(slot)
+        activate(slot + 1)
 
     weights[0].wait()
     moments = Moments()
@@ -312,14 +359,24 @@
     raw[0, rows(0, 1), :] = top
     raw[0, rows(height - 1, 1), :] = bottom
     take_halo(feature_halo())
-    put(0, jnp.maximum(feat[rows(0, 1), :].astype(F32), 0.0))
-    put(height + 1, jnp.maximum(feat[rows(height + 1, 1), :].astype(F32), 0.0))
+    activate(0)
+    activate(height + 1)
     top = raw[0, rows(0, 1), :] + taps(0, 0, 1, (0,))
     bottom = raw[0, rows(height - 1, 1), :] + taps(0, height - 1, 1, (2,))
     for side, row, value in ((0, 0, top), (1, height - 1, bottom)):
         raw[0, rows(row, 1), :] = value
         rim_out[0, side] = value.astype(BF16)
         moments.add(value)
+
+    @pl.when(is_odd)
+    def _():
+        pl.semaphore_wait(barrier, count - 1)
+        pl.semaphore_signal(everyone, inc=1, device_id=partner, device_id_type=LOGICAL)
+
+    @pl.when(is_even)
+    def _():
+        pl.semaphore_wait(everyone, 1)
+
     send_stat(0, moments)
     send_halo(raw_halo(0))
     loads[5].wait()
@@ -368,6 +425,7 @@
         convs, taps, _, width, _ = conv_weight.shape
         assert images == 1 and height % 2 == 0 and height >= 4
         count = imgs * strips
+        assert strips % 2 == 0 and count == 2 ** (count.bit_length() - 1)
         cells = height * cols
         hbm = pl.BlockSpec(memory_space=pltpu.HBM)
         vmem = pl.BlockSpec(memory_space=pltpu.VMEM)
@@ -405,6 +463,8 @@
                 pltpu.SemaphoreType.DMA((convs, 2)),
                 pltpu.SemaphoreType.DMA((convs,)),
                 pltpu.SemaphoreType.DMA((convs,)),
+                pltpu.SemaphoreType.REGULAR,
+                pltpu.SemaphoreType.REGULAR,
             ],
             compiler_params=pltpu.CompilerParams(
                 collective_id=0, has_side_effects=True, vmem_limit_bytes=VMEM_LIMIT

time: 34.8 us -> 32.7 us (0.940)
  Pallas kernels: 33.9 us -> 31.8 us
    pallas_call x1, Pallas kernels: 33.9 us -> 31.8 us  [on_device(): pl.pallas_call(functools.partial(kernel, imgs, strips, height, cols), out...]
where the time goes in v2:
time: 32.7 us; the launch traced here: 32.6 us
  Pallas kernels  31.8 us (97%)
  local copies, waits for them, and re-layouts  0.8 us (2%)
    pallas_call x1, Pallas kernels, on_device(): pl.pallas_call(functools.partial(kernel, imgs, strips, height, cols), out...  31.8 us
    unnamed x1, local copies, waits for them, and re-layouts  0.8 us

profile of v2, /device:TPU:0, one launch (start us, length us, event | category | flops | bytes accessed | tf_op | source)
XLA Modules:
  0.0 32.6 jit_solution(18254789192159004892)
XLA Ops:
  0.0 31.8 %shard_map.64 = bf16[1024,256]{1,0:T(8,128)(2,1)S(1)} custom-call(bf16[1024,1024]{1,0:T(8,128)(2,1)} %bitcast.6, bf16[1024,256]{1,0:T(8,128)(2,1)} %pw_ref.1, f32[1,256]{1,0:T(1,128)} %bitcast.7, bf16[12,768,256]{2,1,0:T(8,128)(2,1)} %bitcast.5, f32[4,256]{1,0:T(4,128)} %gain_ref.1, f32[4,256]{1,0:T(4,128)} %bias_ref.1), custom_call_target="tpu_custom_call" | custom-call | tf_op jit(solution)/shard_map/pallas_call | solution.py:440
  31.8 0.8 %copy.8 = bf16[1,8,128,256]{3,2,1,0:T(8,128)(2,1)} copy(bf16[1,8,128,256]{3,2,1,0:T(8,128)(2,1)S(1)} %bitcast.4) | data formatting | bytes 1048576

commit v3 on v2

--- a/solution.py
+++ b/solution.py
@@ -11,7 +11,8 @@
 LOGICAL = pl.DeviceIdType.LOGICAL
 F32 = jnp.float32
 BF16 = jnp.bfloat16
-STEP = 2
+STEP = 1
+EDGE = 16
 UNROLL = 63
 VMEM_LIMIT = 40 * 1024 * 1024
 
@@ -36,8 +37,7 @@
     pw,
     pb,
     cw,
-    gain,
-    bias,
+    affine,
     feat,
     joined,
     xcat,
@@ -83,20 +83,20 @@
         pltpu.make_async_copy(pw_ref, pw, load_sem.at[0]),
         pltpu.make_async_copy(tokens_ref.at[rows(0, 1)], tok.at[rows(0, 1)], load_sem.at[1]),
         pltpu.make_async_copy(
-            tokens_ref.at[rows(height - 1, 1)], tok.at[rows(1, 1)], load_sem.at[2]
+            tokens_ref.at[rows(height - 1, 1)], tok.at[rows(1, 1)], load_sem.at[1]
         ),
-        pltpu.make_async_copy(pb_ref, pb, load_sem.at[3]),
+        pltpu.make_async_copy(pb_ref, pb, load_sem.at[2]),
         pltpu.make_async_copy(
-            tokens_ref.at[rows(1, height - 2)], tok.at[rows(2, height - 2)], load_sem.at[4]
+            tokens_ref.at[rows(1, height - 2)], tok.at[rows(2, height - 2)], load_sem.at[3]
         ),
-        pltpu.make_async_copy(gain_ref, gain, load_sem.at[5]),
-        pltpu.make_async_copy(bias_ref, bias, load_sem.at[6]),
+        pltpu.make_async_copy(gain_ref, affine.at[0], load_sem.at[4]),
+        pltpu.make_async_copy(bias_ref, affine.at[1], load_sem.at[4]),
     ]
+    rims = pltpu.make_async_copy(tok.at[rows(0, 2)], tok.at[rows(0, 2)], load_sem.at[1])
+    affines = pltpu.make_async_copy(affine, affine, load_sem.at[4])
     weights = [
-        pltpu.make_async_copy(
-            cw_ref.at[pl.ds(3 * k, 3)], cw.at[pl.ds(3 * k, 3)], weight_sem.at[k]
-        )
-        for k in range(4)
+        pltpu.make_async_copy(cw_ref.at[at], cw.at[at], weight_sem.at[i])
+        for i, at in enumerate((pl.ds(0, 3), pl.ds(3, 9)))
     ]
     for load in loads[:4]:
         load.start()
@@ -144,16 +144,18 @@
         for k in range(3):
             rim_in[k, 1] = jnp.zeros((cols, width), BF16)
 
-    column = lax.broadcasted_iota(jnp.int32, (cols, width), 0)
-    at_left, at_right = column == 0, column == cols - 1
+    column = lax.broadcasted_iota(jnp.int32, (EDGE, width), 0)
+    at_left, at_right = column == 0, column == EDGE - 1
+    left, centre, right = (slice(i * width, (i + 1) * width) for i in range(3))
 
     def put(row, value):
-        at = rows(row, 1)
-        xcat[at, 0:width] = jnp.where(at_left, 0.0, pltpu.roll(value, 1, 0)).astype(BF16)
-        xcat[at, width : 2 * width] = value.astype(BF16)
-        xcat[at, 2 * width : 3 * width] = jnp.where(
-            at_right, 0.0, pltpu.roll(value, cols - 1, 0)
-        ).astype(BF16)
+        first, last = row * cols, row * cols + cols - EDGE
+        before, after = pltpu.roll(value, 1, 0), pltpu.roll(value, cols - 1, 0)
+        xcat[pl.ds(first, EDGE), left] = jnp.where(at_left, 0.0, before[:EDGE]).astype(BF16)
+        xcat[pl.ds(first + EDGE, cols - EDGE), left] = before[EDGE:].astype(BF16)
+        xcat[rows(row, 1), centre] = value.astype(BF16)
+        xcat[pl.ds(first, cols - EDGE), right] = after[:-EDGE].astype(BF16)
+        xcat[pl.ds(last, EDGE), right] = jnp.where(at_right, 0.0, after[-EDGE:]).astype(BF16)
 
     def project(slot, number, where):
         value = jnp.dot(tok[rows(slot, number), :], pw[...], preferred_element_type=F32)
@@ -168,16 +170,16 @@
         up = pltpu.make_async_remote_copy(
             src_ref=up_from,
             dst_ref=up_to,
-            send_sem=halo_send.at[phase, 0],
-            recv_sem=halo_recv.at[phase, 1],
+            send_sem=halo_send.at[0],
+            recv_sem=halo_recv.at[phase % 2, 1],
             device_id=above,
             device_id_type=LOGICAL,
         )
         down = pltpu.make_async_remote_copy(
             src_ref=down_from,
             dst_ref=down_to,
-            send_sem=halo_send.at[phase, 1],
-            recv_sem=halo_recv.at[phase, 0],
+            send_sem=halo_send.at[1],
+            recv_sem=halo_recv.at[phase % 2, 0],
             device_id=below,
             device_id_type=LOGICAL,
         )
@@ -219,16 +221,13 @@
         def _():
             up.wait_recv()
 
-    def end_halo(pair):
-        up, down = pair
-
-        @pl.when(has_up)
-        def _():
-            up.wait_send()
-
-        @pl.when(has_down)
-        def _():
-            down.wait_send()
+    def end_halos():
+        for side, there in enumerate((has_up, has_down)):
+
+            @pl.when(there)
+            def _():
+                four = feat.at[rows(0, 4)]
+                pltpu.make_async_copy(four, four, halo_send.at[side]).wait()
 
     def taps(k, first, number, which):
         return sum(
@@ -258,8 +257,8 @@
         return pltpu.make_async_remote_copy(
             src_ref=stats.at[k],
             dst_ref=peers.at[k, distance - 1],
-            send_sem=stat_send.at[k],
-            recv_sem=stat_recv.at[k],
+            send_sem=stat_send,
+            recv_sem=stat_recv.at[k % 2],
             device_id=peer(distance),
             device_id_type=LOGICAL,
         )
@@ -275,7 +274,7 @@
 
     def take_stat(k):
         own = stats[k]
-        pltpu.make_async_copy(peers.at[k], peers.at[k], stat_recv.at[k]).wait()
+        pltpu.make_async_copy(peers.at[k], peers.at[k], stat_recv.at[k % 2]).wait()
         every = peers[k]
         total = jnp.sum(every, axis=0) + own
         even = total[0:1] / count
@@ -284,18 +283,18 @@
         squares = total[1:2] + gaps / cells
         size = cells * count
         average = total[0:1] / size
-        scale = lax.rsqrt(squares / size + epsilon) * gain[k : k + 1, :]
-        return average, scale, bias[k : k + 1, :]
+        scale = lax.rsqrt(squares / size + epsilon) * affine[0, k : k + 1, :]
+        return scale, affine[1, k : k + 1, :] - average * scale
 
     def normed(k, row, norm):
-        average, scale, shift = norm
+        scale, shift = norm
         if row == 0:
             value = rim_in[k, 0].astype(F32)
         elif row == height + 1:
             value = rim_in[k, 1].astype(F32)
         else:
             value = raw[k, rows(row - 1, 1), :]
-        return (value - average) * scale + shift
+        return value * scale + shift
 
     def inside(row, value):
         if row == 0:
@@ -305,7 +304,6 @@
         return value
 
     def conv_stage(k, fill):
-        weights[k].wait()
         moments = Moments()
         filled = 0
         for first in range(0, height, STEP):
@@ -324,10 +322,10 @@
             send_halo(raw_halo(k))
 
     loads[0].wait()
-    loads[1].wait()
-    loads[2].wait()
+    rims.wait()
     loads[3].wait()
-    project(0, 2, (0, height - 1))
+    project(0, 1, (0,))
+    project(1, 1, (height - 1,))
 
     @pl.when(is_even)
     def _():
@@ -343,16 +341,17 @@
     loads[4].wait()
     activate(1)
     activate(height)
-    for slot in range(2, height, 2):
-        project(slot, 2, (slot - 1, slot))
-        activate(slot)
-        activate(slot + 1)
+    half_rows = (height - 2) // 2
+    for slot in (2, 2 + half_rows):
+        project(slot, half_rows, range(slot - 1, slot - 1 + half_rows))
+        for row in range(slot, slot + half_rows):
+            activate(row)
 
     weights[0].wait()
     moments = Moments()
-    for first in range(1, height - 1, 2):
-        value = taps(0, first, 2, range(3))
-        raw[0, rows(first, 2), :] = value
+    for first in (1, 1 + half_rows):
+        value = taps(0, first, half_rows, range(3))
+        raw[0, rows(first, half_rows), :] = value
         moments.add(value)
     top = taps(0, 0, 1, (1, 2))
     bottom = taps(0, height - 1, 1, (0, 1))
@@ -379,8 +378,8 @@
 
     send_stat(0, moments)
     send_halo(raw_halo(0))
-    loads[5].wait()
-    loads[6].wait()
+    affines.wait()
+    weights[1].wait()
 
     def hidden(k):
         norm = take_stat(k)
@@ -410,11 +409,8 @@
         value = joined[rows(row, 1), :].astype(F32) + normed(3, row + 1, norm_3)
         out_ref[rows(row, 1), :] = value.astype(BF16)
 
-    end_halo(feature_halo())
-    for k in range(3):
-        end_halo(raw_halo(k))
-    for k in range(4):
-        pltpu.make_async_copy(peers.at[k], peers.at[k], stat_send.at[k]).wait()
+    end_halos()
+    pltpu.make_async_copy(peers, peers, stat_send).wait()
 
 
 def solution(mesh):
@@ -447,8 +443,7 @@
                 pltpu.VMEM((embed, width), BF16),
                 pltpu.VMEM((1, width), F32),
                 pltpu.VMEM((convs * taps, taps * width, width), BF16),
-                pltpu.VMEM((convs, width), F32),
-                pltpu.VMEM((convs, width), F32),
+                pltpu.VMEM((2, convs, width), F32),
                 pltpu.VMEM((cells + 2 * cols, width), BF16),
                 pltpu.VMEM((cells, width), BF16),
                 pltpu.VMEM((cells + 2 * cols, taps * width), BF16),
@@ -457,12 +452,12 @@
                 pltpu.VMEM((convs - 1, 2, cols, width), BF16),
                 pltpu.VMEM((convs, 2, width), F32),
                 pltpu.VMEM((convs, count - 1, 2, width), F32),
-                pltpu.SemaphoreType.DMA((7,)),
-                pltpu.SemaphoreType.DMA((convs,)),
-                pltpu.SemaphoreType.DMA((convs, 2)),
-                pltpu.SemaphoreType.DMA((convs, 2)),
-                pltpu.SemaphoreType.DMA((convs,)),
-                pltpu.SemaphoreType.DMA((convs,)),
+                pltpu.SemaphoreType.DMA((5,)),
+                pltpu.SemaphoreType.DMA((2,)),
+                pltpu.SemaphoreType.DMA((2,)),
+                pltpu.SemaphoreType.DMA((2, 2)),
+                pltpu.SemaphoreType.DMA,
+                pltpu.SemaphoreType.DMA((2,)),
                 pltpu.SemaphoreType.REGULAR,
                 pltpu.SemaphoreType.REGULAR,
             ],

time: 32.7 us -> 32.1 us (0.982)
  Pallas kernels: 31.8 us -> 31.1 us
    pallas_call x1, Pallas kernels: 31.8 us -> 31.1 us  [on_device(): pl.pallas_call(functools.partial(kernel, imgs, strips, height, cols), out...]
where the time goes in v3:
time: 32.1 us; the launch traced here: 31.9 us
  Pallas kernels  31.1 us (97%)
  local copies, waits for them, and re-layouts  0.8 us (2%)
    pallas_call x1, Pallas kernels, on_device(): pl.pallas_call(functools.partial(kernel, imgs, strips, height, cols), out...  31.1 us
    unnamed x1, local copies, waits for them, and re-layouts  0.8 us

profile of v3, /device:TPU:0, one launch (start us, length us, event | category | flops | bytes accessed | tf_op | source)
XLA Modules:
  0.0 31.9 jit_solution(13617220991165185900)
XLA Ops:
  0.0 31.1 %shard_map.64 = bf16[1024,256]{1,0:T(8,128)(2,1)S(1)} custom-call(bf16[1024,1024]{1,0:T(8,128)(2,1)} %bitcast.6, bf16[1024,256]{1,0:T(8,128)(2,1)} %pw_ref.1, f32[1,256]{1,0:T(1,128)} %bitcast.7, bf16[12,768,256]{2,1,0:T(8,128)(2,1)} %bitcast.5, f32[4,256]{1,0:T(4,128)} %gain_ref.1, f32[4,256]{1,0:T(4,128)} %bias_ref.1), custom_call_target="tpu_custom_call" | custom-call | tf_op jit(solution)/shard_map/pallas_call | solution.py:436
  31.1 0.8 %copy.8 = bf16[1,8,128,256]{3,2,1,0:T(8,128)(2,1)} copy(bf16[1,8,128,256]{3,2,1,0:T(8,128)(2,1)S(1)} %bitcast.4) | data formatting | bytes 1048576
